TPU v7x, 256 devices: a whole 4x4x8 slice. The times are simulated.
256 devices in a mesh: leaf: 256 (over x, z, y, core).
Axes of the slice: x: 4, y: 4, z: 8, core: 2. Of those that a mesh axis runs over, the one named last changes fastest.
Arguments:
- random_block: bfloat16 [131072, 256], P('leaf'), may hold values from -6 to 6
- diag_block: bfloat16 [131072, 512], P('leaf'), may hold values from -0.25 to 0.25
- basis_out: bfloat16 [131072, 256], P('leaf'), may hold values from -0.1875 to 0.1875
- basis_in: bfloat16 [131072, 256], P('leaf'), may hold values from -0.25 to 0.25
- low_up: bfloat16 [256, 5, 256, 256], P('leaf'), as said below
- low_down: bfloat16 [256, 5, 256, 256], P('leaf'), as said below
- low_coupling: bfloat16 [256, 5, 256, 256], P('leaf'), as said below
- top_up: bfloat16 [12, 256, 256], replicated, may hold values from -0.25 to 0.25
- top_down: bfloat16 [12, 256, 256], replicated, may hold values from -0.375 to 0.375
- top_coupling: bfloat16 [14, 256, 256], replicated, may hold values from -0.375 to 0.375
Outputs:
- sample: bfloat16 [131072, 256], P('leaf')
Inputs may be any that keep to these rules, and one draw needn't show every extreme that they name: `low_up`: for every level l below 5, entries [i, l] and [j, l] are the same matrix when i // 2^l == j // 2^l. `low_down`: for every level l below 5, entries [i, l] and [j, l] are the same matrix when i // 2^l == j // 2^l. `low_coupling`: for every level l below 5, entries [i, l] and [j, l] are the same matrix when i // 2^l == j // 2^l.
All inputs are finite; a program needn't handle non-finite values.
Results may differ from a plain program's by a relative error of at most 0.018.
Values may be sent and summed in bfloat16 or wider, within the bound.
A program may use at most 64 MiB of HBM per device.

v0:
```python
import jax
import jax.numpy as jnp
from jax import lax
from jax.sharding import PartitionSpec as P

TOP = 3


def as_sent(x):
    return jax.tree.map(lambda a: a.astype(jnp.bfloat16) if a.dtype == jnp.float32 else a, x)


def swapped(block, axis, stride):
    count = lax.axis_size(axis)
    route = []
    for low in range(count):
        high = low | 1 << stride
        if high != low and high < count:
            route += [(low, high), (high, low)]
    return lax.ppermute(block, axis, route)


def apply_left(matrix, values):
    return jnp.dot(matrix, values, preferred_element_type=jnp.float32)


def apply_trans(matrix, values):
    return lax.dot_general(
        matrix, values, (((0,), (0,)), ((), ())), preferred_element_type=jnp.float32
    )


def exchange_sibling(payload, height):
    return jax.tree.map(
        lambda part, own: part.astype(own.dtype), swapped(as_sent(payload), "leaf", height), payload
    )


def pick_node(table, position):
    return lax.dynamic_index_in_dim(table, position, 0, keepdims=False)


def per_device(
    random_block,
    diag_block,
    basis_out,
    basis_in,
    low_up,
    low_down,
    low_coupling,
    top_up,
    top_down,
    top_coupling,
):
    low_levels = low_up.shape[1]
    device = lax.axis_index("leaf")
    current = apply_trans(basis_in, random_block)
    lower_terms = []
    for height in range(low_levels):
        rounded = current.astype(jnp.bfloat16)
        lifted = apply_trans(low_up[0, height], rounded).astype(jnp.bfloat16)
        sibling_state, sibling_lift = exchange_sibling((rounded, lifted), height)
        lower_terms.append(apply_left(low_coupling[0, height], sibling_state))
        current = lifted.astype(jnp.float32) + sibling_lift.astype(jnp.float32)
    upper_terms = []
    for section in range(TOP):
        height = low_levels + section
        offset = 2 ** (TOP + 1) - 2 ** (TOP + 1 - section)
        own_node = jnp.right_shift(device, height)
        rounded = current.astype(jnp.bfloat16)
        coupler = pick_node(top_coupling, offset + own_node)
        if section < TOP - 1:
            lifter = pick_node(top_up, offset + own_node)
            lifted = apply_trans(lifter, rounded).astype(jnp.bfloat16)
            sibling_state, sibling_lift = exchange_sibling((rounded, lifted), height)
            current = lifted.astype(jnp.float32) + sibling_lift.astype(jnp.float32)
        else:
            (sibling_state,) = exchange_sibling((rounded,), height)
        upper_terms.append(apply_left(coupler, sibling_state))
    descent = upper_terms[-1]
    for section in range(TOP - 2, -1, -1):
        height = low_levels + section
        offset = 2 ** (TOP + 1) - 2 ** (TOP + 1 - section)
        own_node = jnp.right_shift(device, height)
        lowering = pick_node(top_down, offset + own_node)
        descent = apply_left(lowering, descent.astype(jnp.bfloat16)) + upper_terms[section]
    for height in range(low_levels - 1, -1, -1):
        descent = (
            apply_left(low_down[0, height], descent.astype(jnp.bfloat16)) + lower_terms[height]
        )
    local = apply_left(diag_block, random_block)
    spread = apply_left(basis_out, descent.astype(jnp.bfloat16))
    return (local + spread).astype(jnp.bfloat16)


def solution(mesh):
    placed = (
        P("leaf", None),
        P("leaf", None),
        P("leaf", None),
        P("leaf", None),
        P("leaf", None, None, None),
        P("leaf", None, None, None),
        P("leaf", None, None, None),
        P(),
        P(),
        P(),
    )
    return jax.shard_map(
        per_device, mesh=mesh, in_specs=placed, out_specs=P("leaf", None), check_vma=False
    )
```

profile of v0, /device:TPU:0, one launch (start us, length us, event | category | flops | bytes accessed | tf_op | source)
XLA Modules:
  0.0 94.2 jit_solution(13626321482972888122)
XLA Ops:
  0.0 2.1 %convolution_convert_fusion = bf16[256,256]{1,0:T(8,128)(2,1)} fusion(bf16[512,256]{1,0:T(8,128)(2,1)} %param.13, bf16[512,256]{1,0:T(8,128)(2,1)} %param.10), kind=kOutput, calls=%fused_computation.17 | convolution fusion | flops 67174400 | bytes 655360 | tf_op jit(solution)/shard_map/dot_general | solution.py:28
  3.4 1.3 %collective-permute-done = bf16[256,256]{0,1:T(8,128)(2,1)S(1)} collective-permute-done((bf16[256,256]{0,1:T(8,128)(2,1)S(1)}, bf16[256,256]{0,1:T(8,128)(2,1)S(1)}, u32[]{:S(2)}, u32[]{:S(2)}) %collective-permute-start) | collective-permute-done | bytes 131104 | tf_op jit(solution)/shard_map/ppermute | solution.py:20
  6.7 5.5 %collective-permute-done.1 = bf16[256,256]{0,1:T(8,128)(2,1)S(1)} collective-permute-done((bf16[256,256]{0,1:T(8,128)(2,1)S(1)}, bf16[256,256]{0,1:T(8,128)(2,1)S(1)}, u32[]{:S(2)}, u32[]{:S(2)}) %collective-permute-start.1) | collective-permute-done | bytes 131104 | tf_op jit(solution)/shard_map/ppermute | solution.py:20
  14.0 1.6 %collective-permute-start.2 = (bf16[256,256]{0,1:T(8,128)(2,1)S(1)}, bf16[256,256]{0,1:T(8,128)(2,1)S(1)}, u32[]{:S(2)}, u32[]{:S(2)}) collective-permute-start(bf16[256,256]{0,1:T(8,128)(2,1)S(1)} %fusion.17), channel_id=1, source_target_pairs={{0,4},{4,0},{1,5},{5,1},{2,6},{6,2},{3,7},{7,3},{8,12},{12,8},{9,1... | collective-permute-start | bytes 393224 | tf_op jit(solution)/shard_map/ppermute | solution.py:20
  15.6 5.0 %collective-permute-done.2 = bf16[256,256]{0,1:T(8,128)(2,1)S(1)} collective-permute-done((bf16[256,256]{0,1:T(8,128)(2,1)S(1)}, bf16[256,256]{0,1:T(8,128)(2,1)S(1)}, u32[]{:S(2)}, u32[]{:S(2)}) %collective-permute-start.2) | collective-permute-done | bytes 131104 | tf_op jit(solution)/shard_map/ppermute | solution.py:20
  22.6 4.8 %collective-permute-done.3 = bf16[256,256]{0,1:T(8,128)(2,1)S(1)} collective-permute-done((bf16[256,256]{0,1:T(8,128)(2,1)S(1)}, bf16[256,256]{0,1:T(8,128)(2,1)S(1)}, u32[]{:S(2)}, u32[]{:S(2)}) %collective-permute-start.3) | collective-permute-done | bytes 131104 | tf_op jit(solution)/shard_map/ppermute | solution.py:20
  28.1 1.6 %collective-permute-start.4 = (bf16[256,256]{0,1:T(8,128)(2,1)S(1)}, bf16[256,256]{0,1:T(8,128)(2,1)S(1)}, u32[]{:S(2)}, u32[]{:S(2)}) collective-permute-start(bf16[256,256]{0,1:T(8,128)(2,1)S(1)} %fusion.19), channel_id=1, source_target_pairs={{0,16},{16,0},{1,17},{17,1},{2,18},{18,2},{3,19},{19,3},{4,20},{20... | collective-permute-start | bytes 393224 | tf_op jit(solution)/shard_map/ppermute | solution.py:20
  29.7 5.7 %collective-permute-done.4 = bf16[256,256]{0,1:T(8,128)(2,1)S(1)} collective-permute-done((bf16[256,256]{0,1:T(8,128)(2,1)S(1)}, bf16[256,256]{0,1:T(8,128)(2,1)S(1)}, u32[]{:S(2)}, u32[]{:S(2)}) %collective-permute-start.4) | collective-permute-done | bytes 131104 | tf_op jit(solution)/shard_map/ppermute | solution.py:20
  37.2 5.7 %collective-permute-start.5 = (bf16[256,256]{1,0:T(8,128)(2,1)S(1)}, bf16[256,256]{1,0:T(8,128)(2,1)S(1)}, u32[]{:S(2)}, u32[]{:S(2)}) collective-permute-start(bf16[256,256]{1,0:T(8,128)(2,1)S(1)} %convolution_convert_fusion.3), channel_id=1, source_target_pairs={{0,32},{32,0},{1,33},{33,1},{2,34},{34,2},{3,35},{35,3},{4,36},{36... | collective-permute-start | bytes 393224 | tf_op jit(solution)/shard_map/ppermute | solution.py:20
  42.9 3.3 %collective-permute-done.5 = bf16[256,256]{1,0:T(8,128)(2,1)S(1)} collective-permute-done((bf16[256,256]{1,0:T(8,128)(2,1)S(1)}, bf16[256,256]{1,0:T(8,128)(2,1)S(1)}, u32[]{:S(2)}, u32[]{:S(2)}) %collective-permute-start.5) | collective-permute-done | bytes 131104 | tf_op jit(solution)/shard_map/ppermute | solution.py:20
  48.7 3.8 %collective-permute-done.6 = bf16[256,256]{1,0:T(8,128)(2,1)S(1)} collective-permute-done((bf16[256,256]{1,0:T(8,128)(2,1)S(1)}, bf16[256,256]{1,0:T(8,128)(2,1)S(1)}, u32[]{:S(2)}, u32[]{:S(2)}) %collective-permute-start.6) | collective-permute-done | bytes 131104 | tf_op jit(solution)/shard_map/ppermute | solution.py:20
  52.5 3.1 %collective-permute-start.7 = (bf16[256,256]{1,0:T(8,128)(2,1)S(1)}, bf16[256,256]{1,0:T(8,128)(2,1)S(1)}, u32[]{:S(2)}, u32[]{:S(2)}) collective-permute-start(bf16[256,256]{1,0:T(8,128)(2,1)S(1)} %add_convert_fusion), channel_id=1, source_target_pairs={{0,128},{128,0},{1,129},{129,1},{2,130},{130,2},{3,131},{131,3},{4... | collective-permute-start | bytes 393224 | tf_op jit(solution)/shard_map/ppermute | solution.py:20
  55.6 1.3 %fusion.89 = f32[512,256]{1,0:T(8,128)S(1)} fusion(bf16[512,512]{1,0:T(8,128)(2,1)} %param.11, bf16[512,256]{1,0:T(8,128)(2,1)S(1)} %copy-done.1), kind=kOutput, calls=%fused_computation.94 | convolution fusion | flops 134217728 | bytes 1310720 | tf_op jit(solution)/shard_map/dot_general | solution.py:24
  57.0 2.0 %collective-permute-start.13 = (bf16[256,256]{0,1:T(8,128)(2,1)}, bf16[256,256]{0,1:T(8,128)(2,1)}, u32[]{:S(2)}, u32[]{:S(2)}) collective-permute-start(bf16[256,256]{0,1:T(8,128)(2,1)} %add_convert_fusion.6), channel_id=1, source_target_pairs={{0,2},{2,0},{1,3},{3,1},{4,6},{6,4},{5,7},{7,5},{8,10},{10,8},{9,1... | collective-permute-start | bytes 393224 | tf_op jit(solution)/shard_map/ppermute | solution.py:20
  59.0 2.9 %collective-permute-start.12 = (bf16[256,256]{0,1:T(8,128)(2,1)}, bf16[256,256]{0,1:T(8,128)(2,1)}, u32[]{:S(2)}, u32[]{:S(2)}) collective-permute-start(bf16[256,256]{0,1:T(8,128)(2,1)} %add_convert_fusion.5), channel_id=1, source_target_pairs={{0,4},{4,0},{1,5},{5,1},{2,6},{6,2},{3,7},{7,3},{8,12},{12,8},{9,1... | collective-permute-start | bytes 393224 | tf_op jit(solution)/shard_map/ppermute | solution.py:20
  64.1 2.8 %collective-permute-done.8 = bf16[256,256]{1,0:T(8,128)(2,1)} collective-permute-done((bf16[256,256]{1,0:T(8,128)(2,1)S(1)}, bf16[256,256]{1,0:T(8,128)(2,1)}, u32[]{:S(2)}, u32[]{:S(2)}) %collective-permute-start.8) | collective-permute-done | bytes 131104 | tf_op jit(solution)/shard_map/ppermute | solution.py:20
  66.9 5.9 %collective-permute-start.9 = (bf16[256,256]{0,1:T(8,128)(2,1)}, bf16[256,256]{0,1:T(8,128)(2,1)}, u32[]{:S(2)}, u32[]{:S(2)}) collective-permute-start(bf16[256,256]{0,1:T(8,128)(2,1)} %add_convert_fusion.2), channel_id=1, source_target_pairs={{0,32},{32,0},{1,33},{33,1},{2,34},{34,2},{3,35},{35,3},{4,36},{36... | collective-permute-start | bytes 393224 | tf_op jit(solution)/shard_map/ppermute | solution.py:20
  72.9 1.4 %fusion.14 = f32[256,256]{1,0:T(8,128)S(1)} fusion(f32[256,256]{1,0:T(8,128)S(1)} %fusion.20, bf16[256,256]{1,0:T(8,128)(2,1)} %collective-permute-done.8, bf16[14,256,256]{2,1,0:T(8,128)(2,1)S(1)} %copy-done, s32[]{:T(128)S(6)} %select_n.22, bf16[12,256,256]{2,1,0:T(8,128)(2,1)} %param.18, s32[]{:T(128)S(6)} %select_n.19), kind=kOutput, calls=%fused_computation.31 | convolution fusion | flops 67239936 | bytes 917512 | tf_op jit(solution)/shard_map/dot_general | solution.py:24
  74.2 3.4 %collective-permute-done.9 = bf16[256,256]{0,1:T(8,128)(2,1)} collective-permute-done((bf16[256,256]{0,1:T(8,128)(2,1)}, bf16[256,256]{0,1:T(8,128)(2,1)}, u32[]{:S(2)}, u32[]{:S(2)}) %collective-permute-start.9) | collective-permute-done | bytes 131104 | tf_op jit(solution)/shard_map/ppermute | solution.py:20
  77.7 4.2 %collective-permute-start.10 = (bf16[256,256]{0,1:T(8,128)(2,1)}, bf16[256,256]{0,1:T(8,128)(2,1)}, u32[]{:S(2)}, u32[]{:S(2)}) collective-permute-start(bf16[256,256]{0,1:T(8,128)(2,1)} %copy-done.4), channel_id=1, source_target_pairs={{0,16},{16,0},{1,17},{17,1},{2,18},{18,2},{3,19},{19,3},{4,20},{20... | collective-permute-start | bytes 393224 | tf_op jit(solution)/shard_map/ppermute | solution.py:20
  81.9 1.4 %fusion.13 = f32[256,256]{1,0:T(8,128)S(1)} fusion(f32[256,256]{1,0:T(8,128)S(1)} %fusion.14, bf16[256,256]{0,1:T(8,128)(2,1)} %collective-permute-done.9, bf16[1,5,256,256]{3,2,1,0:T(8,128)(2,1)S(1)} %copy-done.3, bf16[14,256,256]{2,1,0:T(8,128)(2,1)S(1)} %copy-done, s32[]{:T(128)S(6)} %select_n.23), kind=kOutput, calls=%fused_computation.30 | convolution fusion | flops 67239936 | bytes 917508 | tf_op jit(solution)/shard_map/dot_general | solution.py:24
  83.2 3.3 %collective-permute-done.10 = bf16[256,256]{0,1:T(8,128)(2,1)} collective-permute-done((bf16[256,256]{0,1:T(8,128)(2,1)}, bf16[256,256]{0,1:T(8,128)(2,1)}, u32[]{:S(2)}, u32[]{:S(2)}) %collective-permute-start.10) | collective-permute-done | bytes 131104 | tf_op jit(solution)/shard_map/ppermute | solution.py:20
  87.9 1.3 %fusion.11 = f32[256,256]{1,0:T(8,128)S(1)} fusion(f32[256,256]{1,0:T(8,128)S(1)} %fusion.12, bf16[256,256]{0,1:T(8,128)(2,1)} %collective-permute-done.11, bf16[1,5,256,256]{3,2,1,0:T(8,128)(2,1)S(1)} %copy-done.3, bf16[1,5,256,256]{3,2,1,0:T(8,128)(2,1)} %param.16), kind=kOutput, calls=%fused_computation.28 | convolution fusion | flops 67239936 | bytes 917504 | tf_op jit(solution)/shard_map/dot_general | solution.py:24
  91.9 2.3 %fusion.1 = bf16[512,256]{1,0:T(8,128)(2,1)} fusion(f32[512,256]{1,0:T(8,128)S(1)} %fusion.89, bf16[512,256]{1,0:T(8,128)(2,1)} %param.12, f32[256,256]{1,0:T(8,128)S(1)} %fusion.9, bf16[256,256]{1,0:T(8,128)(2,1)} %collective-permute-done.14, bf16[1,5,256,256]{3,2,1,0:T(8,128)(2,1)} %param.16), kind=kOutput, calls=%fused_computation.2 | convolution fusion | flops 101056512 | bytes 1572864 | tf_op jit(solution)/shard_map/dot_general | solution.py:24
  (40 shorter events, 18.3 us)
Async XLA Ops:
  0.0 62.8 %copy-start = (bf16[14,256,256]{2,1,0:T(8,128)(2,1)S(1)}, bf16[14,256,256]{2,1,0:T(8,128)(2,1)}, u32[]{:S(2)}) copy-start(bf16[14,256,256]{2,1,0:T(8,128)(2,1)} %param.19) | copy-start | bytes 5505028
  0.0 12.9 %copy-start.2 = (bf16[1,5,256,256]{3,2,1,0:T(8,128)(2,1)S(1)}, bf16[1,5,256,256]{3,2,1,0:T(8,128)(2,1)}, u32[]{:S(2)}) copy-start(bf16[1,5,256,256]{3,2,1,0:T(8,128)(2,1)} %param.14) | copy-start | bytes 1966084
  3.3 1.4 %collective-permute-start = (bf16[256,256]{0,1:T(8,128)(2,1)S(1)}, bf16[256,256]{0,1:T(8,128)(2,1)S(1)}, u32[]{:S(2)}, u32[]{:S(2)}) collective-permute-start(bf16[256,256]{0,1:T(8,128)(2,1)S(1)} %fusion.15), channel_id=1, source_target_pairs={{0,1},{1,0},{2,3},{3,2},{4,5},{5,4},{6,7},{7,6},{8,9},{9,8},{10,11... | collective-permute-start | bytes 393224 | tf_op jit(solution)/shard_map/ppermute | solution.py:20
  6.6 5.6 %collective-permute-start.1 = (bf16[256,256]{0,1:T(8,128)(2,1)S(1)}, bf16[256,256]{0,1:T(8,128)(2,1)S(1)}, u32[]{:S(2)}, u32[]{:S(2)}) collective-permute-start(bf16[256,256]{0,1:T(8,128)(2,1)S(1)} %fusion.16), channel_id=1, source_target_pairs={{0,2},{2,0},{1,3},{3,1},{4,6},{6,4},{5,7},{7,5},{8,10},{10,8},{9,1... | collective-permute-start | bytes 393224 | tf_op jit(solution)/shard_map/ppermute | solution.py:20
  14.0 41.6 %copy-start.1 = (bf16[512,256]{1,0:T(8,128)(2,1)S(1)}, bf16[512,256]{1,0:T(8,128)(2,1)}, u32[]{:S(2)}) copy-start(bf16[512,256]{1,0:T(8,128)(2,1)} %param.10) | copy-start | bytes 786436
  14.0 6.6 %collective-permute-start.2 = (bf16[256,256]{0,1:T(8,128)(2,1)S(1)}, bf16[256,256]{0,1:T(8,128)(2,1)S(1)}, u32[]{:S(2)}, u32[]{:S(2)}) collective-permute-start(bf16[256,256]{0,1:T(8,128)(2,1)S(1)} %fusion.17), channel_id=1, source_target_pairs={{0,4},{4,0},{1,5},{5,1},{2,6},{6,2},{3,7},{7,3},{8,12},{12,8},{9,1... | collective-permute-start | bytes 393224 | tf_op jit(solution)/shard_map/ppermute | solution.py:20
  22.4 5.1 %collective-permute-start.3 = (bf16[256,256]{0,1:T(8,128)(2,1)S(1)}, bf16[256,256]{0,1:T(8,128)(2,1)S(1)}, u32[]{:S(2)}, u32[]{:S(2)}) collective-permute-start(bf16[256,256]{0,1:T(8,128)(2,1)S(1)} %fusion.18), channel_id=1, source_target_pairs={{0,8},{8,0},{1,9},{9,1},{2,10},{10,2},{3,11},{11,3},{4,12},{12,4},... | collective-permute-start | bytes 393224 | tf_op jit(solution)/shard_map/ppermute | solution.py:20
  27.4 0.6 copy-start.4
  28.1 7.3 %collective-permute-start.4 = (bf16[256,256]{0,1:T(8,128)(2,1)S(1)}, bf16[256,256]{0,1:T(8,128)(2,1)S(1)}, u32[]{:S(2)}, u32[]{:S(2)}) collective-permute-start(bf16[256,256]{0,1:T(8,128)(2,1)S(1)} %fusion.19), channel_id=1, source_target_pairs={{0,16},{16,0},{1,17},{17,1},{2,18},{18,2},{3,19},{19,3},{4,20},{20... | collective-permute-start | bytes 393224 | tf_op jit(solution)/shard_map/ppermute | solution.py:20
  37.2 9.0 %collective-permute-start.5 = (bf16[256,256]{1,0:T(8,128)(2,1)S(1)}, bf16[256,256]{1,0:T(8,128)(2,1)S(1)}, u32[]{:S(2)}, u32[]{:S(2)}) collective-permute-start(bf16[256,256]{1,0:T(8,128)(2,1)S(1)} %convolution_convert_fusion.3), channel_id=1, source_target_pairs={{0,32},{32,0},{1,33},{33,1},{2,34},{34,2},{3,35},{35,3},{4,36},{36... | collective-permute-start | bytes 393224 | tf_op jit(solution)/shard_map/ppermute | solution.py:20
  46.2 35.6 %copy-start.3 = (bf16[1,5,256,256]{3,2,1,0:T(8,128)(2,1)S(1)}, bf16[1,5,256,256]{3,2,1,0:T(8,128)(2,1)}, u32[]{:S(2)}) copy-start(bf16[1,5,256,256]{3,2,1,0:T(8,128)(2,1)} %param.15) | copy-start | bytes 1966084
  47.5 5.1 %collective-permute-start.6 = (bf16[256,256]{1,0:T(8,128)(2,1)S(1)}, bf16[256,256]{1,0:T(8,128)(2,1)S(1)}, u32[]{:S(2)}, u32[]{:S(2)}) collective-permute-start(bf16[256,256]{1,0:T(8,128)(2,1)S(1)} %convolution_convert_fusion.2), channel_id=1, source_target_pairs={{0,64},{64,0},{1,65},{65,1},{2,66},{66,2},{3,67},{67,3},{4,68},{68... | collective-permute-start | bytes 393224 | tf_op jit(solution)/shard_map/ppermute | solution.py:20
  48.7 43.2 %collective-permute-start.14 = (bf16[256,256]{1,0:T(8,128)(2,1)}, bf16[256,256]{1,0:T(8,128)(2,1)}, u32[]{:S(2)}, u32[]{:S(2)}) collective-permute-start(bf16[256,256]{1,0:T(8,128)(2,1)} %convolution_convert_fusion), channel_id=1, source_target_pairs={{0,1},{1,0},{2,3},{3,2},{4,5},{5,4},{6,7},{7,6},{8,9},{9,8},{10,11... | collective-permute-start | bytes 393224 | tf_op jit(solution)/shard_map/ppermute | solution.py:20
  52.5 9.3 %collective-permute-start.7 = (bf16[256,256]{1,0:T(8,128)(2,1)S(1)}, bf16[256,256]{1,0:T(8,128)(2,1)S(1)}, u32[]{:S(2)}, u32[]{:S(2)}) collective-permute-start(bf16[256,256]{1,0:T(8,128)(2,1)S(1)} %add_convert_fusion), channel_id=1, source_target_pairs={{0,128},{128,0},{1,129},{129,1},{2,130},{130,2},{3,131},{131,3},{4... | collective-permute-start | bytes 393224 | tf_op jit(solution)/shard_map/ppermute | solution.py:20
  57.0 33.6 %collective-permute-start.13 = (bf16[256,256]{0,1:T(8,128)(2,1)}, bf16[256,256]{0,1:T(8,128)(2,1)}, u32[]{:S(2)}, u32[]{:S(2)}) collective-permute-start(bf16[256,256]{0,1:T(8,128)(2,1)} %add_convert_fusion.6), channel_id=1, source_target_pairs={{0,2},{2,0},{1,3},{3,1},{4,6},{6,4},{5,7},{7,5},{8,10},{10,8},{9,1... | collective-permute-start | bytes 393224 | tf_op jit(solution)/shard_map/ppermute | solution.py:20
  59.0 30.3 %collective-permute-start.12 = (bf16[256,256]{0,1:T(8,128)(2,1)}, bf16[256,256]{0,1:T(8,128)(2,1)}, u32[]{:S(2)}, u32[]{:S(2)}) collective-permute-start(bf16[256,256]{0,1:T(8,128)(2,1)} %add_convert_fusion.5), channel_id=1, source_target_pairs={{0,4},{4,0},{1,5},{5,1},{2,6},{6,2},{3,7},{7,3},{8,12},{12,8},{9,1... | collective-permute-start | bytes 393224 | tf_op jit(solution)/shard_map/ppermute | solution.py:20
  61.9 26.0 %collective-permute-start.11 = (bf16[256,256]{0,1:T(8,128)(2,1)}, bf16[256,256]{0,1:T(8,128)(2,1)}, u32[]{:S(2)}, u32[]{:S(2)}) collective-permute-start(bf16[256,256]{0,1:T(8,128)(2,1)} %add_convert_fusion.4), channel_id=1, source_target_pairs={{0,8},{8,0},{1,9},{9,1},{2,10},{10,2},{3,11},{11,3},{4,12},{12,4},... | collective-permute-start | bytes 393224 | tf_op jit(solution)/shard_map/ppermute | solution.py:20
  61.9 5.1 %collective-permute-start.8 = (bf16[256,256]{1,0:T(8,128)(2,1)S(1)}, bf16[256,256]{1,0:T(8,128)(2,1)}, u32[]{:S(2)}, u32[]{:S(2)}) collective-permute-start(bf16[256,256]{1,0:T(8,128)(2,1)S(1)} %add_convert_fusion.1), channel_id=1, source_target_pairs={{0,64},{64,0},{1,65},{65,1},{2,66},{66,2},{3,67},{67,3},{4,68},{68... | collective-permute-start | bytes 393224 | tf_op jit(solution)/shard_map/ppermute | solution.py:20
  66.9 10.7 %collective-permute-start.9 = (bf16[256,256]{0,1:T(8,128)(2,1)}, bf16[256,256]{0,1:T(8,128)(2,1)}, u32[]{:S(2)}, u32[]{:S(2)}) collective-permute-start(bf16[256,256]{0,1:T(8,128)(2,1)} %add_convert_fusion.2), channel_id=1, source_target_pairs={{0,32},{32,0},{1,33},{33,1},{2,34},{34,2},{3,35},{35,3},{4,36},{36... | collective-permute-start | bytes 393224 | tf_op jit(solution)/shard_map/ppermute | solution.py:20
  77.7 8.9 %collective-permute-start.10 = (bf16[256,256]{0,1:T(8,128)(2,1)}, bf16[256,256]{0,1:T(8,128)(2,1)}, u32[]{:S(2)}, u32[]{:S(2)}) collective-permute-start(bf16[256,256]{0,1:T(8,128)(2,1)} %copy-done.4), channel_id=1, source_target_pairs={{0,16},{16,0},{1,17},{17,1},{2,18},{18,2},{3,19},{19,3},{4,20},{20... | collective-permute-start | bytes 393224 | tf_op jit(solution)/shard_map/ppermute | solution.py:20
where the time goes:
time: 94.6 us; the launch traced here: 94.2 us
  waiting for transfers between devices  39 us (41%)
  starting transfers between devices  29.6 us (31%)
  matrix products  22.1 us (23%)
  other arithmetic  2.84 us (3%)
    ppermute x15, waiting for transfers between devices, swapped(): return lax.ppermute(block, axis, route)  39 us
    ppermute x15, starting transfers between devices, swapped(): return lax.ppermute(block, axis, route)  29.6 us
    dot_general x9, matrix products, apply_left(): return jnp.dot(matrix, values, preferred_element_type=jnp.float32)  13 us
    dot_general x8, matrix products, apply_trans(): lax.dot_general(matrix, values, (((0,), (0,)), ((), ())), preferred_eleme...  9.19 us
    convert_element_type x7, other arithmetic, per_device(): rounded = current.astype(jnp.bfloat16)  2.84 us
  transfers between devices with their start and end apart: 15, of which 10 were waited for; matrix products, arithmetic and copies ran while one was open for 11% of the time, Pallas kernels for 0%

commit v1 on v0

v1 whole, which is shorter than its diff:
```python
import jax
import jax.numpy as jnp
from jax import lax
from jax.experimental import pallas as pl
from jax.experimental.pallas import tpu as pltpu
from jax.sharding import PartitionSpec as P

BF = jnp.bfloat16
F32 = jnp.float32
ROWS = 32


def mm(a, b):
    return jnp.dot(a, b, preferred_element_type=F32)


def mmt(a, b):
    return lax.dot_general(a, b, (((1,), (1,)), ((), ())), preferred_element_type=F32)


def body(
    x_h, d_h, u_h, v_h, lw_h, lr_h, lb_h, tw_h, tr_h, tb_h,
    out,
    x_v, d_v, u_v, v_v, w_v, r_v, b_v, tw_v, tr_v, tb_v,
    c0, c0s, p1, p1r, p3, yrecv, c3, p4, p4r, c3r, zrecv, xrecv,
    c1h, p2h, p2r, c2h, c1s, c2s, zall, base, k5, k6, ka, kb, ur,
    load_sem, send_sem, recv_sem,
):
    me = lax.axis_index("leaf")
    core = me % 2
    y = (me // 2) % 4
    z = (me // 8) % 8
    x = me // 64
    p = me % 8
    zl = z % 4
    zh = z // 4

    def dev(xx, zz, yy, cc):
        return ((xx * 8 + zz) * 4 + yy) * 2 + cc

    y_peers = [
        (dev(x, z, (y + dy) % 4, (core + dc) % 2), ((y + dy) % 4) * 2 + (core + dc) % 2)
        for dy, dc in ((2, 0), (2, 1), (1, 0), (3, 0), (1, 1), (3, 1), (0, 1))
    ]
    y_from = [
        ((y - dy + 4) % 4) * 2 + (core + dc) % 2
        for dy, dc in ((2, 0), (2, 1), (1, 0), (3, 0), (1, 1), (3, 1), (0, 1))
    ]
    z_peers = [dev(x, (z + dz) % 8, y, core) for dz in (4, 3, 5, 2, 6, 1, 7)]
    x_peers = [dev((x + dx) % 4, z, y, core) for dx in (2, 1, 3)]
    mate = dev(x, z, y, 1 - core)
    y1 = dev(x, z, y + 1 - 2 * (y % 2), core)
    y2 = dev(x, z, (y + 2) % 4, core)

    barrier = pltpu.get_barrier_semaphore()
    peers = [q[0] for q in y_peers] + z_peers + x_peers
    for peer in peers:
        pl.semaphore_signal(barrier, inc=1, device_id=(peer,), device_id_type=pl.DeviceIdType.MESH)

    loads = {}

    def load(name, src, dst):
        k = len(loads)
        loads[name] = pltpu.make_async_copy(src, dst, load_sem.at[k])
        loads[name].start()

    n5, n6, n7 = me // 32, me // 64, me // 128
    load("x", x_h, x_v)
    load("v", v_h, v_v)
    for l in range(3):
        load(f"w{l}", lw_h.at[0, l], w_v.at[l])
    for l in range(3, 5):
        load(f"w{l}", lw_h.at[0, l], w_v.at[l])
    sib5 = n5 + 1 - 2 * (n5 % 2)
    far = (1 - n7) * 2
    load("w5o", tw_h.at[n5], tw_v.at[0])
    load("w5s", tw_h.at[sib5], tw_v.at[1])
    load("w6a", tw_h.at[8 + far], tw_v.at[2])
    load("w6b", tw_h.at[8 + far + 1], tw_v.at[3])
    load("r5", tr_h.at[n5], tr_v.at[0])
    load("r6", tr_h.at[8 + n6], tr_v.at[1])
    load("b5", tb_h.at[n5], tb_v.at[0])
    load("b6", tb_h.at[8 + n6], tb_v.at[1])
    load("b7", tb_h.at[12 + n7], tb_v.at[2])
    load("r", lr_h.at[0], r_v)
    load("b", lb_h.at[0], b_v)
    load("u", u_h, u_v)
    load("d", d_h, d_v)

    sent = []

    def copy(src, dst, k, peer):
        return pltpu.make_async_remote_copy(
            src_ref=src, dst_ref=dst, send_sem=send_sem.at[k], recv_sem=recv_sem.at[k],
            device_id=(peer,), device_id_type=pl.DeviceIdType.MESH,
        )

    def send(src, dst, k, peer):
        c = copy(src, dst, k, peer)
        c.start()
        sent.append(c)
        return c

    loads["x"].wait()
    loads["v"].wait()
    c0[...] = lax.dot_general(
        x_v[...], v_v[...], (((0,), (0,)), ((), ())), preferred_element_type=F32
    ).astype(BF)
    loads["w0"].wait()
    p1[...] = mm(c0[...], w_v[0]).astype(BF).reshape(2, 128, 256)
    loads["w1"].wait()
    p2 = mm(p1[...].reshape(256, 256), w_v[1]).astype(BF)
    loads["w2"].wait()
    p3[...] = mm(p2, w_v[2]).astype(BF).reshape(8, ROWS, 256)

    pl.semaphore_wait(barrier, len(peers))

    y_up = [send(p3.at[q], yrecv.at[i], i, peer) for i, (peer, q) in enumerate(y_peers)]
    m_c0 = send(c0, c0s, 7, mate)
    m_p1 = send(p1.at[1 - core], p1r, 8, mate)

    for n in ("w3", "w4", "w5o", "w5s", "w6a", "w6b", "r5", "r6", "b5", "b6", "b7", "r", "b"):
        loads[n].wait()
    r4 = r_v[4]
    r5 = tr_v[0]
    k5[...] = mm(r4, tb_v[0]).astype(BF)
    t = mm(r5, tb_v[1]).astype(BF)
    k6[...] = mm(r4, t).astype(BF)
    t = mm(tr_v[1], tb_v[2]).astype(BF)
    t = mm(r5, t).astype(BF)
    t = mm(r4, t).astype(BF)
    ka[...] = mmt(t, tw_v[2]).astype(BF)
    kb[...] = mmt(t, tw_v[3]).astype(BF)

    m_p1.wait_recv()
    half = (p1[core].astype(F32) + p1r[...].astype(F32)).astype(BF)
    c1h[...] = half
    p2h[...] = mm(half, w_v[1]).astype(BF)

    for c in y_up:
        c.wait_recv()
    total = p3[p].astype(F32)
    for i in range(7):
        total += yrecv[i].astype(F32)
    c3v = total.astype(BF)
    c3[...] = c3v
    p4v = mm(c3v, w_v[3]).astype(BF)
    p4[...] = p4v
    zrecv[z] = mm(p4v, w_v[4]).astype(BF)

    z_up = [send(zrecv.at[z], zrecv.at[z], 9 + i, peer) for i, peer in enumerate(z_peers)]
    cousin = zh * 4 + (1 - zl // 2) * 2
    s4 = [
        send(p4, p4r.at[zl % 2], 16 + i, dev(x, cousin + (zl + i) % 2, y, core)) for i in range(2)
    ]
    s3 = send(c3, c3r, 18, dev(x, z + 1 - 2 * (z % 2), y, core))
    s_c1 = send(c1h, c1s.at[core], 19, y1)
    s_p2 = send(p2h, p2r, 20, y1)

    loads["u"].wait()
    loads["d"].wait()
    base[...] = mm(d_v[...], x_v[...])
    ur[...] = mm(u_v[...], r_v[0]).astype(BF)
    m_c0.wait_recv()
    f0 = mmt(c0s[...], b_v[0]).astype(BF)
    base[...] += mmt(u_v[...], f0)

    s_p2.wait_recv()
    c2h[...] = (p2h[...].astype(F32) + p2r[...].astype(F32)).astype(BF)
    s_c2 = send(c2h, c2s.at[core], 21, y2)
    s_c1.wait_recv()
    m_c1 = send(c1s.at[core], c1s.at[core], 22, mate)

    for c in z_up:
        c.wait_recv()
    own = zrecv[zh * 4].astype(F32)
    sib = zrecv[(1 - zh) * 4].astype(F32)
    for j in range(1, 4):
        own += zrecv[zh * 4 + j].astype(F32)
        sib += zrecv[(1 - zh) * 4 + j].astype(F32)
    c5o = own.astype(BF)
    c5s = sib.astype(BF)
    xrecv[x] = (mm(c5o, tw_v[0]) + mm(c5s, tw_v[1])).astype(BF)
    x_up = [send(xrecv.at[x], xrecv.at[x], 23 + i, peer) for i, peer in enumerate(x_peers)]

    for c in s4:
        c.wait_recv()
    c4s = (p4r[0].astype(F32) + p4r[1].astype(F32)).astype(BF)
    pre4 = mmt(c5s, k5[...]) + mmt(c4s, b_v[4])
    s3.wait_recv()
    f3 = mmt(c3r[...], b_v[3])

    for c in x_up:
        c.wait_recv()
    near = x + 1 - 2 * (x % 2)
    xfar = (1 - x // 2) * 2
    v4 = pre4 + mmt(xrecv[near], k6[...]) + mmt(xrecv[xfar], ka[...]) + mmt(xrecv[xfar + 1], kb[...])
    zall[p] = (mmt(v4.astype(BF), r_v[3]) + f3).astype(BF)
    z_dn = [send(zall.at[p], zall.at[p], 26 + i, peer) for i, (peer, q) in enumerate(y_peers)]

    s_c2.wait_recv()
    m_c2 = send(c2s.at[core], c2s.at[core], 33, mate)
    m_c1.wait_recv()
    f1 = mmt(c1s[...].reshape(256, 256), b_v[1])
    m_c2.wait_recv()
    f2 = mmt(c2s[...].reshape(256, 256), b_v[2])

    for c in z_dn:
        c.wait_recv()
    z3 = zall[...].reshape(256, 256)
    z2 = (mmt(z3, r_v[2]) + f2).astype(BF)
    z1 = (mmt(z2, r_v[1]) + f1).astype(BF)
    out[...] = (base[...] + mmt(ur[...], z1)).astype(BF)

    for c in sent:
        c.wait_send()


def per_device(*args):
    any_spec = pl.BlockSpec(memory_space=pltpu.HBM)
    sq = (256, 256)
    vm = lambda *s: pltpu.VMEM(s, BF)
    return pl.pallas_call(
        body,
        out_shape=jax.ShapeDtypeStruct((512, 256), BF),
        in_specs=[any_spec] * 10,
        out_specs=pl.BlockSpec(memory_space=pltpu.VMEM),
        scratch_shapes=[
            vm(512, 256), vm(512, 512), vm(512, 256), vm(512, 256),
            vm(5, *sq), vm(5, *sq), vm(5, *sq), vm(4, *sq), vm(2, *sq), vm(3, *sq),
            vm(*sq), vm(*sq), vm(2, 128, 256), vm(128, 256), vm(8, ROWS, 256), vm(7, ROWS, 256),
            vm(ROWS, 256), vm(ROWS, 256), vm(2, ROWS, 256), vm(ROWS, 256), vm(8, ROWS, 256),
            vm(4, ROWS, 256),
            vm(128, 256), vm(128, 256), vm(128, 256), vm(128, 256), vm(2, 128, 256), vm(2, 128, 256),
            vm(8, ROWS, 256), pltpu.VMEM((512, 256), F32),
            vm(*sq), vm(*sq), vm(*sq), vm(*sq), vm(512, 256),
            pltpu.SemaphoreType.DMA((24,)),
            pltpu.SemaphoreType.DMA((34,)),
            pltpu.SemaphoreType.DMA((34,)),
        ],
        compiler_params=pltpu.CompilerParams(
            collective_id=0, has_side_effects=True, vmem_limit_bytes=66000000
        ),
        name="hss",
    )(*args)


def solution(mesh):
    placed = (
        P("leaf", None),
        P("leaf", None),
        P("leaf", None),
        P("leaf", None),
        P("leaf", None, None, None),
        P("leaf", None, None, None),
        P("leaf", None, None, None),
        P(),
        P(),
        P(),
    )
    return jax.shard_map(
        per_device, mesh=mesh, in_specs=placed, out_specs=P("leaf", None), check_vma=False
    )
```

time: 94.6 us -> 31.7 us (0.34)
  the two profiles are of different devices: /device:TPU:0 before, /device:TPU:1 now
where the time goes in v1:
time: 31.7 us; the launch traced here: 31.6 us
  Pallas kernels  29.9 us (94%)
  local copies, waits for them, and re-layouts  1.67 us (5%)
    pallas_call x1, Pallas kernels, per_device(): pl.pallas_call(body, out_shape=jax.ShapeDtypeStruct((512, 256), BF), in_s...  29.9 us
    unnamed x1, local copies, waits for them, and re-layouts  1.67 us

profile of v1, /device:TPU:1, one launch (start us, length us, event | category | flops | bytes accessed | tf_op | source)
XLA Modules:
  0.0 31.6 jit_solution(9346825296911342117)
XLA Ops:
  0.0 29.9 %hss.1 = bf16[512,256]{1,0:T(8,128)(2,1)} custom-call(bf16[512,256]{1,0:T(8,128)(2,1)} %x_h.1, bf16[512,512]{1,0:T(8,128)(2,1)} %d_h.1, bf16[512,256]{1,0:T(8,128)(2,1)} %u_h.1, bf16[512,256]{1,0:T(8,128)(2,1)} %v_h.1, bf16[1,5,256,256]{3,2,1,0:T(8,128)(2,1)} %lw_h.1, bf16[1,5,256,256]{3,2,1,0:T(8,128)(2,1)} %lr_h.1, bf16[1,5,256,256]{3,2,1,0:T(8,128)(2,1)} %lb_h.1, ...), custom_call_target="tpu_custom_call" | custom-call | tf_op jit(solution)/shard_map/hss/pallas_call | solution.py:223
  29.9 1.7 %copy.12 = bf16[512,256]{1,0:T(8,128)(2,1)} copy(bf16[512,256]{1,0:T(8,128)(2,1)} %hss.1) | data formatting | bytes 524288
